TPU v7x, 32 devices: a whole 2x2x4 slice. The times are simulated.
32 devices in a mesh: batch: 4 (over x, core), seq: 8 (over z, y).
Axes of the slice: x: 2, y: 2, z: 4, core: 2. Of those that a mesh axis runs over, the one named last changes fastest.
Arguments:
- query: bfloat16 [8, 64, 128], P('batch'), may hold values from -300 to 300
- cache_keys: bfloat16 [8, 16384, 512], P('batch', 'seq'), may hold values from -6 to 6
- cache_values: bfloat16 [8, 16384, 512], P('batch', 'seq'), may hold values from -6 to 6
- new_keys: bfloat16 [8, 512], P('batch'), may hold values from -6 to 6
- new_values: bfloat16 [8, 512], P('batch'), may hold values from -6 to 6
- key_up: bfloat16 [512, 1024], P('seq'), may hold values from -0.25 to 0.25
- value_up: bfloat16 [512, 1024], P('seq'), may hold values from -0.25 to 0.25
- out_weight: bfloat16 [8192, 8192], P('seq', 'batch'), may hold values from -0.5 to 0.5
- lengths: int32 [8], P('batch'), may hold values from 128 to 16384, as said below
Outputs:
- mixed: bfloat16 [8, 8192], P('seq', 'batch')
Inputs may be any that keep to these rules, and one draw needn't show every extreme that they name: `lengths`: every length is a multiple of 128, at least 128; some sequence fills all 16384 slots. Slots at or beyond a sequence's length hold arbitrary finite entries that must not affect the result.
All inputs are finite; a program needn't handle non-finite values.
Results may differ from a plain program's by a relative error of at most 0.019.
Values may be sent and summed in bfloat16 or wider, within the bound.
A program may use at most 64 MiB of HBM per device.

v0:
```python
import jax
import jax.numpy as jnp
from jax import lax
from jax.sharding import PartitionSpec as P

NEGATIVE = -1e30
TOP_PRECISION = lax.Precision.HIGHEST


def body(
    query, cache_keys, cache_values, new_keys, new_values, key_up, value_up, out_weight, lengths
):
    batch_rows, cache_len, rank_full = cache_keys.shape
    head_count, head_dimension = (query.shape[1], query.shape[2])
    kv_heads = key_up.shape[1] // head_dimension
    group_size = head_count // kv_heads
    score_scale_factor = head_dimension ** (-0.5)
    seq_index = lax.axis_index("seq")
    seq_count = lax.axis_size("seq")
    local_head_index = head_count // seq_count
    positions = seq_index * cache_len + lax.iota(jnp.int32, cache_len)
    live_mask = (positions[None, :] < lengths[:, None])[:, None, None, :]
    grouped = query.reshape(batch_rows, kv_heads, group_size, head_dimension)
    key_full, value_full = (
        lax.all_gather(key_up, "seq", axis=0, tiled=True),
        lax.all_gather(value_up, "seq", axis=0, tiled=True),
    )
    rebuilt_keys = jnp.dot(
        cache_keys.reshape(batch_rows * cache_len, rank_full),
        key_full,
        preferred_element_type=jnp.float32,
    ).reshape(batch_rows, cache_len, kv_heads, head_dimension)
    rebuilt_values = jnp.dot(
        cache_values.reshape(batch_rows * cache_len, rank_full),
        value_full,
        preferred_element_type=jnp.float32,
    ).reshape(batch_rows, cache_len, kv_heads, head_dimension)
    expanded_query = grouped.astype(jnp.float32)
    scores = (
        jnp.einsum("bkgd,blkd->bkgl", expanded_query, rebuilt_keys, precision=TOP_PRECISION)
        * score_scale_factor
    )
    fresh_key_row = jnp.dot(new_keys, key_full, preferred_element_type=jnp.float32).reshape(
        batch_rows, kv_heads, head_dimension
    )
    current_token_score = (
        jnp.einsum("phsu,phu->phs", expanded_query, fresh_key_row, precision=TOP_PRECISION)
        * score_scale_factor
    )
    new_value = jnp.dot(new_values, value_full, preferred_element_type=jnp.float32).reshape(
        batch_rows, kv_heads, head_dimension
    )
    scores = jnp.where(live_mask, scores, NEGATIVE)
    local_max = jnp.max(scores, axis=-1)
    upper_limit = jnp.maximum(lax.pmax(local_max, "seq"), current_token_score)
    softmax_terms = jnp.where(live_mask, jnp.exp(scores - upper_limit[..., None]), 0.0)
    denominator = jnp.sum(softmax_terms, axis=-1)
    totals = jnp.einsum("bkgl,blkd->bkgd", softmax_terms, rebuilt_values, precision=TOP_PRECISION)
    denominator, totals = (
        lax.psum(denominator.astype(jnp.bfloat16), "seq").astype(jnp.float32),
        lax.psum(totals.astype(jnp.bfloat16), "seq").astype(jnp.float32),
    )
    own_weight = jnp.exp(current_token_score - upper_limit)
    normalized = (totals + own_weight[..., None] * new_value[:, :, None, :]) / (
        denominator + own_weight
    )[..., None]
    normalized = normalized.reshape(batch_rows, head_count * head_dimension)
    width_local = local_head_index * head_dimension
    attended = lax.dynamic_slice_in_dim(normalized, seq_index * width_local, width_local, 1).astype(
        jnp.bfloat16
    )
    partial_out = jnp.dot(
        lax.all_gather(attended, "batch", axis=0, tiled=True),
        out_weight,
        preferred_element_type=jnp.float32,
    )
    return lax.psum_scatter(
        partial_out.astype(jnp.bfloat16), "seq", scatter_dimension=0, tiled=True
    )


def solution(mesh):
    placed = (
        P("batch", None, None),
        P("batch", "seq", None),
        P("batch", "seq", None),
        P("batch", None),
        P("batch", None),
        P("seq", None),
        P("seq", None),
        P("seq", "batch"),
        P("batch"),
    )
    return jax.shard_map(
        body, mesh=mesh, in_specs=placed, out_specs=P("seq", "batch"), check_vma=False
    )
```

profile of v0, /device:TPU:0, one launch (start us, length us, event | category | flops | bytes accessed | tf_op | source)
XLA Modules:
  0.0 230.1 jit_solution(15584377831851506746)
XLA Ops:
  6.5 0.0 copy-start
  6.5 0.0 all-gather.6.cloned.1.call-start
  6.5 0.7 all-gather.6.cloned.1.call-update
  7.3 0.0 all-gather.4.cloned.1.call-start
  7.3 0.7 all-gather.4.cloned.1.call-update
  8.0 1.3 dynamic-slice
  9.3 0.7 broadcast_compare_fusion
  10.0 42.5 %all-gather.6.cloned.1.call-done = bf16[512,1024]{1,0:T(8,128)(2,1)} async-done(((bf16[64,1024]{1,0:T(8,128)(2,1)}), bf16[512,1024]{1,0:T(8,128)(2,1)}) %all-gather.6.cloned.1.call-update) | async-done | bytes 1048592 | tf_op jit(solution)/shard_map/all_gather | solution.py:26
  52.5 1.5 convolution_bitcast_fusion
  54.0 39.7 %all-gather.4.cloned.1.call-done = bf16[512,1024]{1,0:T(8,128)(2,1)} async-done(((bf16[64,1024]{1,0:T(8,128)(2,1)}), bf16[512,1024]{1,0:T(8,128)(2,1)}) %all-gather.4.cloned.1.call-update) | async-done | bytes 1048592 | tf_op jit(solution)/shard_map/all_gather | solution.py:25
  93.7 0.0 copy-start.1
  93.7 1.6 convolution_bitcast_fusion.1
  95.3 1.5 copy.18
  96.8 1.5 copy.16
  98.3 0.0 copy-done
  98.3 0.2 fusion.12
  98.5 0.0 copy-done.1
  98.5 4.5 %fusion.2 = f32[2,2048,8,128]{3,1,2,0:T(8,128)S(1)} fusion(bf16[2,2048,512]{2,1,0:T(8,128)(2,1)S(1)} %copy-done.1, bf16[8,128,512,1]{1,0,2,3:T(8,128)(2,1)S(1)} %bitcast.67), kind=kOutput, calls=%fused_computation.2 | convolution fusion | flops 4294967296 | bytes 22020096 | tf_op jit(solution)/shard_map/dot_general | solution.py:28
  103.0 7.7 %fusion.17 = (f32[2,8,8]{2,1,0:T(8,128)S(1)}, f32[2,8,8,2048]{3,2,1,0:T(8,128)S(1)}) fusion(f32[2,2048,8,128]{3,1,2,0:T(8,128)S(1)} %fusion.2, bf16[2,64,128]{2,1,0:T(8,128)(2,1)S(1)} %copy-done, pred[2,2048]{1,0:T(4,128)(4,1)S(1)} %broadcast_compare_fusion), kind=kOutput, calls=%fused_computation.34 | convolution fusion | flops 403439488 | bytes 17863168 | tf_op jit(solution)/shard_map/bkgd,blkd->bkgl/dot_general | solution.py:40
  110.7 19.5 %pmax.7 = f32[2,8,8]{2,1,0:T(8,128)S(1)} all-reduce(f32[2,8,8]{2,1,0:T(8,128)S(1)} %get-tuple-element.9), channel_id=1, replica_groups=mesh['batch'=4,'seq'=8] {'seq'}, use_global_device_ids=true, to_apply=%region_1.2 | all-reduce | flops 128 | bytes 1024 | tf_op jit(solution)/shard_map/pmax | solution.py:55
  130.3 0.3 fusion.8
  130.6 6.3 %fusion = f32[2,2048,8,128]{3,1,2,0:T(8,128)S(1)} fusion(bf16[2,2048,512]{2,1,0:T(8,128)(2,1)} %param.11, bf16[8,128,512,1]{1,0,2,3:T(8,128)(2,1)S(1)} %bitcast.66), kind=kOutput, calls=%fused_computation | convolution fusion | flops 4294967296 | bytes 22020096 | tf_op jit(solution)/shard_map/dot_general | solution.py:33
  136.9 8.6 %convolution_convert_fusion.1 = bf16[2,8,8,128]{3,2,1,0:T(8,128)(2,1)S(1)} fusion(f32[2,2048,8,128]{3,1,2,0:T(8,128)S(1)} %fusion, f32[2,8,8,2048]{3,2,1,0:T(8,128)S(1)} %get-tuple-element.10, f32[2,8,8]{2,1,0:T(8,128)S(1)} %multiply_maximum_fusion, pred[2,2048]{1,0:T(4,128)(4,1)S(1)} %broadcast_compare_fusion), kind=kOutput, calls=%fused_computation.8 | convolution fusion | flops 403193856 | bytes 17863168 | tf_op jit(solution)/shard_map/bkgl,blkd->bkgd/dot_general | solution.py:58
  145.6 33.4 %all-reduce.1 = (bf16[2,8,8,128]{3,2,1,0:T(8,128)(2,1)S(1)}, bf16[2,8,8]{2,1,0:T(8,128)(2,1)S(1)}) all-reduce(bf16[2,8,8,128]{3,2,1,0:T(8,128)(2,1)S(1)} %convolution_convert_fusion.1, bf16[2,8,8]{2,1,0:T(8,128)(2,1)S(1)} %fusion.8), channel_id=1, replica_groups=mesh['batch'=4,'seq'=8] {'seq'}, use_global_device_ids=true, to_apply=%region_2.3 | all-reduce | flops 16512 | bytes 66048 | tf_op jit(solution)/shard_map/psum | solution.py:61
  178.9 0.1 divide_bitcast_fusion
  179.1 5.2 %all-gather = bf16[4,2,1024]{2,1,0:T(2,128)(2,1)S(1)} all-gather(bf16[1,2,1024]{2,1,0:T(2,128)(2,1)S(1)} %fusion.15), channel_id=1, replica_groups=mesh['batch'=4,'seq'=8] {'batch'}, dimensions={0}, use_global_device_ids=true | all-gather | bytes 20480 | tf_op jit(solution)/shard_map/all_gather | solution.py:73
  184.4 2.8 %convolution_convert_fusion = bf16[8,2048]{1,0:T(8,128)(2,1)S(1)} fusion(bf16[8,1024]{1,0:T(8,128)(2,1)S(1)} %reshape.54, bf16[1024,2048]{1,0:T(8,128)(2,1)} %param.16), kind=kOutput, calls=%fused_computation.7 | convolution fusion | flops 33570816 | bytes 4243456 | tf_op jit(solution)/shard_map/dot_general | solution.py:72
  187.2 34.9 %all-reduce = bf16[8,2048]{1,0:T(8,128)(2,1)S(1)} all-reduce(bf16[8,2048]{1,0:T(8,128)(2,1)S(1)} %convolution_convert_fusion), channel_id=2, replica_groups=mesh['batch'=4,'seq'=8] {'seq'}, use_global_device_ids=true, to_apply=%region_5.6.clone | all-reduce | flops 16384 | bytes 65536
  222.1 1.2 constant_dynamic-slice_fusion
  (8 shorter events, 0.1 us)
Async XLA Ops:
  6.5 91.8 %copy-start = (bf16[2,64,128]{2,1,0:T(8,128)(2,1)S(1)}, bf16[2,64,128]{2,1,0:T(8,128)(2,1)}, u32[]{:S(2)}) copy-start(bf16[2,64,128]{2,1,0:T(8,128)(2,1)} %param.9) | copy-start | bytes 98308
  6.5 46.0 %all-gather.6.cloned.1.call-start = ((), (), s32[]{:S(2)}) async-start(), calls=%async_computation.1 | async-start | bytes 1179648 | tf_op jit(solution)/shard_map/all_gather | solution.py:26
  7.3 86.4 %all-gather.4.cloned.1.call-start = ((), (), s32[]{:S(2)}) async-start(), calls=%async_computation | async-start | bytes 1179648 | tf_op jit(solution)/shard_map/all_gather | solution.py:25
  93.7 4.9 %copy-start.1 = (bf16[2,2048,512]{2,1,0:T(8,128)(2,1)S(1)}, bf16[2,2048,512]{2,1,0:T(8,128)(2,1)}, u32[]{:S(2)}) copy-start(bf16[2,2048,512]{2,1,0:T(8,128)(2,1)} %param.10) | copy-start | bytes 12582916
Sparse Core Ops, SparseCore 0:
  9.5 42.9 all-gather.5
  54.6 38.9 all-gather.3
where the time goes:
time: 230 us
  blocking collectives  93 us (40%)
  waiting for transfers between devices  83.6 us (36%)
  matrix products  33.3 us (14%)
  between operations  13.5 us (6%)
  local copies, waits for them, and re-layouts  5.55 us (2%)
    all_gather x1, waiting for transfers between devices, body(): lax.all_gather(value_up, 'seq', axis=0, tiled=True)  42.5 us
    all_gather x1, waiting for transfers between devices, body(): lax.all_gather(key_up, 'seq', axis=0, tiled=True)  39.7 us
    unnamed x1, blocking collectives  34.9 us
    psum x1, blocking collectives, body(): lax.psum(totals.astype(jnp.bfloat16), 'seq').astype(jnp.float32)  33.4 us
    pmax x1, blocking collectives, body(): upper_limit = jnp.maximum(lax.pmax(local_max, 'seq'), current_token_score)  19.5 us
    dot_general x1, matrix products, body(): jnp.einsum('bkgl,blkd->bkgd', softmax_terms, rebuilt_values, precision=TO...  8.63 us
    dot_general x1, matrix products, body(): jnp.einsum('bkgd,blkd->bkgl', expanded_query, rebuilt_keys, precision=TOP...  7.68 us
    dot_general x1, matrix products, body(): jnp.dot(cache_values.reshape(batch_rows * cache_len, rank_full), value_fu...  6.31 us
  transfers between devices with their start and end apart: 2, of which 2 were waited for; matrix products, arithmetic and copies ran while one was open for 2% of the time, Pallas kernels for 0%

commit v1 on v0

--- a/solution.py
+++ b/solution.py
@@ -1,10 +1,287 @@
+import functools
+
 import jax
 import jax.numpy as jnp
 from jax import lax
+from jax.experimental import pallas as pl
+from jax.experimental.pallas import tpu as pltpu
 from jax.sharding import PartitionSpec as P
 
 NEGATIVE = -1e30
 TOP_PRECISION = lax.Precision.HIGHEST
+MESH = pl.DeviceIdType.MESH
+NT = (((1,), (1,)), ((), ()))
+NN = (((1,), (0,)), ((), ()))
+F32 = jnp.float32
+BF16 = jnp.bfloat16
+
+
+def split_halves(x):
+    head = x.astype(BF16)
+    rest = (x - head.astype(F32)).astype(BF16)
+    return jnp.concatenate([head, rest], axis=0)
+
+
+def split_dot(x, y, dims):
+    rows = x.shape[0]
+    both = lax.dot_general(split_halves(x), y, dims, preferred_element_type=F32)
+    return both[:rows] + both[rows:]
+
+
+def step_kernel(
+    ns, nb, lengths, query, keys, values, new_k, new_v, key_up, value_up, out_w, out,
+    kbuf, vbuf, wbuf, qin, ku, nk, nv, qs, qfull, vcol, os, orecv, mls, mlrecv, att, ps, pr,
+    lsem, qsend, qrecv, vsend, vrecv, osend, orcv, msend, mrcv, asend, arcv, psend, prcv,
+):
+    me = lax.axis_index("seq")
+    mb = lax.axis_index("batch")
+    seqs, heads, dh = qin.shape
+    cache_len = kbuf.shape[1]
+    rl = ku.shape[0]
+    hl = heads // ns
+    kv = ku.shape[1] // dh
+    group = heads // kv
+    rows = seqs * hl
+    scale = dh ** (-0.5)
+
+    local = [
+        pltpu.make_async_copy(query, qin, lsem.at[0]),
+        pltpu.make_async_copy(key_up, ku, lsem.at[1]),
+        pltpu.make_async_copy(new_k, nk, lsem.at[2]),
+        pltpu.make_async_copy(new_v, nv, lsem.at[3]),
+        pltpu.make_async_copy(
+            value_up.at[:, pl.ds(pl.multiple_of(me * dh, 128), dh)],
+            vcol.at[pl.ds(pl.multiple_of(me * rl, 8), rl)],
+            lsem.at[4],
+        ),
+        pltpu.make_async_copy(keys.at[0], kbuf.at[0], lsem.at[5]),
+        pltpu.make_async_copy(keys.at[1], kbuf.at[1], lsem.at[6]),
+        pltpu.make_async_copy(values.at[0], vbuf.at[0], lsem.at[7]),
+        pltpu.make_async_copy(values.at[1], vbuf.at[1], lsem.at[8]),
+        pltpu.make_async_copy(out_w, wbuf, lsem.at[9]),
+    ]
+    for copy in local:
+        copy.start()
+
+    barrier = pltpu.get_barrier_semaphore()
+    for d in range(1, ns):
+        pl.semaphore_signal(
+            barrier, inc=1, device_id={"seq": lax.rem(me + d, ns)}, device_id_type=MESH
+        )
+    for d in range(1, nb):
+        pl.semaphore_signal(
+            barrier, inc=1, device_id={"batch": lax.rem(mb + d, nb)}, device_id_type=MESH
+        )
+
+    local[0].wait()
+    local[1].wait()
+    low = lax.broadcasted_iota(jnp.int32, (group, 2 * rl), 1) < rl
+    for k in range(kv):
+        part = ku[:, k * dh : (k + 1) * dh]
+        twice = jnp.concatenate([part, part], axis=0)
+        asked = jnp.concatenate(
+            [qin[b, k * group : (k + 1) * group, :].astype(F32) for b in range(seqs)], axis=0
+        ).astype(BF16)
+        got = lax.dot_general(asked, twice, NT, preferred_element_type=F32)
+        qs[me, k * group : (k + 1) * group, :] = jnp.where(low, got[:group], got[group:])
+
+    pl.semaphore_wait(barrier, ns - 1 + nb - 1)
+
+    def hop(src, dst, send, recv, d, axis, target):
+        return pltpu.make_async_remote_copy(
+            src_ref=src, dst_ref=dst, send_sem=send.at[d], recv_sem=recv.at[d],
+            device_id={axis: target}, device_id_type=MESH,
+        )
+
+    started = []
+
+    def send_all(count, index, axis, src_of, dst, send, recv):
+        for d in range(1, count):
+            target = lax.rem(index + d, count)
+            copy = hop(src_of(target), dst(index), send, recv, d, axis, target)
+            copy.start()
+            started.append(copy)
+
+    def receive(count, index, axis, src_of, dst, send, recv, d):
+        source = lax.rem(index + count - d, count)
+        hop(src_of(source), dst(source), send, recv, d, axis, source).wait_recv()
+
+    q_args = (ns, me, "seq", lambda t: qs.at[me], lambda s: qs.at[s], qsend, qrecv)
+    send_all(*q_args)
+
+    for d in range(1, ns):
+        receive(*q_args, d)
+
+    v_args = (
+        ns, me, "seq",
+        lambda t: value_up.at[:, pl.ds(pl.multiple_of(t * dh, 128), dh)],
+        lambda s: vcol.at[pl.ds(pl.multiple_of(s * rl, 8), rl)],
+        vsend, vrecv,
+    )
+    send_all(*v_args)
+
+    wide = lax.broadcasted_iota(jnp.int32, (heads, 2 * rl), 1) < rl
+    for pair in range(ns // 2):
+        even, odd = qs[2 * pair], qs[2 * pair + 1]
+        lanes = slice(pair * 2 * rl, (pair + 1) * 2 * rl)
+        qfull[0, :, lanes] = jnp.where(wide, even, pltpu.roll(odd, rl, 1))
+        qfull[1, :, lanes] = jnp.where(wide, pltpu.roll(even, rl, 1), odd)
+
+    positions = me * cache_len + lax.broadcasted_iota(jnp.int32, (1, cache_len), 1)
+    sums, tops, totals = [], [], []
+    for b in range(seqs):
+        live = positions < lengths[b]
+        local[5 + b].wait()
+        scores = split_dot(qfull[b], kbuf[b], NT) * scale
+        scores = jnp.where(live, scores, NEGATIVE)
+        top = jnp.max(scores, axis=1, keepdims=True)
+        terms = jnp.where(live, jnp.exp(scores - top), 0.0)
+        tops.append(top)
+        totals.append(jnp.sum(terms, axis=1, keepdims=True))
+        local[7 + b].wait()
+        sums.append(split_dot(terms, vbuf[b], NN))
+
+    quarter = lax.broadcasted_iota(jnp.int32, (hl, 128), 1) // 32
+    for p in range(ns):
+        span = slice(p * hl, (p + 1) * hl)
+        os[p] = jnp.concatenate([x[span] for x in sums], axis=0).astype(BF16)
+        mls[p] = jnp.where(
+            quarter == 0, tops[0][span],
+            jnp.where(
+                quarter == 1, totals[0][span],
+                jnp.where(quarter == 2, tops[1][span], totals[1][span]),
+            ),
+        )
+    m_args = (ns, me, "seq", lambda t: mls.at[t], lambda s: mlrecv.at[s], msend, mrcv)
+    o_args = (ns, me, "seq", lambda t: os.at[t], lambda s: orecv.at[s], osend, orcv)
+    send_all(*m_args)
+    send_all(*o_args)
+
+    local[2].wait()
+    local[3].wait()
+    local[4].wait()
+    mine = pl.ds(pl.multiple_of(me * hl, 8), hl)
+    own_query = jnp.concatenate([qfull[b, mine, :] for b in range(seqs)], axis=0)
+
+    def spread(ref):
+        full = ref[...].astype(F32)
+        return jnp.concatenate(
+            [jnp.broadcast_to(full[b : b + 1], (hl, full.shape[1])) for b in range(seqs)], axis=0
+        )
+
+    own = jnp.sum(own_query * spread(nk), axis=1, keepdims=True) * scale
+    fresh = spread(nv)
+
+    def stats(x):
+        return (
+            jnp.concatenate([x[:, 0:1], x[:, 64:65]], axis=0),
+            jnp.concatenate([x[:, 32:33], x[:, 96:97]], axis=0),
+        )
+
+    parts = [stats(mls[me])]
+    for d in range(1, ns):
+        receive(*m_args, d)
+        parts.append(stats(mlrecv[lax.rem(me + ns - d, ns)]))
+    limit = own
+    for top, _ in parts:
+        limit = jnp.maximum(limit, top)
+    own_weight = jnp.exp(own - limit)
+    latent = own_weight * fresh
+    below = own_weight
+    for d, (top, total) in enumerate(parts):
+        factor = jnp.exp(top - limit)
+        below = below + factor * total
+        if d:
+            receive(*o_args, d)
+            block = orecv[lax.rem(me + ns - d, ns)]
+        else:
+            block = os[me]
+        latent = latent + factor * block.astype(F32)
+    for d in range(1, ns):
+        receive(*v_args, d)
+    attended = split_dot(latent, vcol[...], NN) / below
+    att[pl.ds(pl.multiple_of(mb * rows, 8), rows), :] = attended.astype(BF16).astype(F32)
+
+    def att_rows(i):
+        return att.at[pl.ds(pl.multiple_of(i * rows, 8), rows)]
+
+    a_args = (nb, mb, "batch", lambda t: att_rows(mb), att_rows, asend, arcv)
+    send_all(*a_args)
+    for d in range(1, nb):
+        receive(*a_args, d)
+    features = jnp.concatenate(
+        [att[pl.ds(g, nb * seqs, stride=hl), :] for g in range(hl)], axis=1
+    ).astype(BF16)
+    local[9].wait()
+    product = lax.dot_general(features, wbuf[...], NN, preferred_element_type=F32)
+    for p in range(ns):
+        ps[p] = product[p : p + 1]
+    p_args = (ns, me, "seq", lambda t: ps.at[t], lambda s: pr.at[s], psend, prcv)
+    send_all(*p_args)
+    result = ps[me]
+    for d in range(1, ns):
+        receive(*p_args, d)
+        result = result + pr[lax.rem(me + ns - d, ns)]
+    out[...] = result.astype(out.dtype)
+    for copy in started:
+        copy.wait_send()
+
+
+def fused_body(
+    query, cache_keys, cache_values, new_keys, new_values, key_up, value_up, out_weight, lengths
+):
+    ns, nb = lax.axis_size("seq"), lax.axis_size("batch")
+    seqs, cache_len, rank = cache_keys.shape
+    heads, dh = query.shape[1:]
+    hl = heads // ns
+    width = out_weight.shape[1]
+    sem = pltpu.SemaphoreType.DMA
+    hbm = pl.BlockSpec(memory_space=pl.ANY)
+    return pl.pallas_call(
+        functools.partial(step_kernel, ns, nb),
+        out_shape=jax.ShapeDtypeStruct((1, width), BF16),
+        in_specs=[pl.BlockSpec(memory_space=pltpu.SMEM)] + [hbm] * 8,
+        out_specs=pl.BlockSpec(memory_space=pltpu.VMEM),
+        scratch_shapes=[
+            pltpu.VMEM(cache_keys.shape, BF16),
+            pltpu.VMEM(cache_values.shape, BF16),
+            pltpu.VMEM(out_weight.shape, BF16),
+            pltpu.VMEM(query.shape, BF16),
+            pltpu.VMEM(key_up.shape, BF16),
+            pltpu.VMEM(new_keys.shape, BF16),
+            pltpu.VMEM(new_values.shape, BF16),
+            pltpu.VMEM((ns, heads, seqs * key_up.shape[0]), F32),
+            pltpu.VMEM((seqs, heads, rank), F32),
+            pltpu.VMEM((rank, dh), BF16),
+            pltpu.VMEM((ns, seqs * hl, rank), BF16),
+            pltpu.VMEM((ns, seqs * hl, rank), BF16),
+            pltpu.VMEM((ns, hl, 128), F32),
+            pltpu.VMEM((ns, hl, 128), F32),
+            pltpu.VMEM((nb * seqs * hl, dh), F32),
+            pltpu.VMEM((ns, 1, width), F32),
+            pltpu.VMEM((ns, 1, width), F32),
+            sem((10,)),
+        ]
+        + [sem((ns,))] * 8
+        + [sem((nb,))] * 2
+        + [sem((ns,))] * 2,
+        compiler_params=pltpu.CompilerParams(collective_id=0, has_side_effects=True),
+        name="decode_step",
+    )(
+        lengths, query, cache_keys, cache_values, new_keys, new_values, key_up, value_up, out_weight
+    )
+
+
+def fits(mesh, query, cache_keys, key_up):
+    ns, nb = mesh.shape["seq"], mesh.shape["batch"]
+    heads, dh = query.shape[1:]
+    kv = key_up.shape[1] // dh
+    seqs = query.shape[0] // nb
+    return (
+        seqs == 2 and kv == ns and heads // kv == 8 and dh == 128
+        and key_up.shape[0] // ns == 64 and query.shape[0] == ns
+        and cache_keys.shape[1] // ns * cache_keys.shape[2] <= 2 ** 21
+    )
 
 
 def body(
@@ -91,6 +368,11 @@
         P("seq", "batch"),
         P("batch"),
     )
-    return jax.shard_map(
-        body, mesh=mesh, in_specs=placed, out_specs=P("seq", "batch"), check_vma=False
-    )
+
+    def run(*args):
+        chosen = fused_body if fits(mesh, args[0], args[1], args[5]) else body
+        return jax.shard_map(
+            chosen, mesh=mesh, in_specs=placed, out_specs=P("seq", "batch"), check_vma=False
+        )(*args)
+
+    return run

time: 230 us -> 33.4 us (0.15)
  blocking collectives: 93 us -> 0 us
  waiting for transfers between devices: 83.6 us -> 0 us
  matrix products: 33.3 us -> 0 us
  Pallas kernels: 0 us -> 31.9 us
  between operations: 13.5 us -> 0.01 us
  local copies, waits for them, and re-layouts: 5.55 us -> 1.3 us
    all_gather x2 -> x0, waiting for transfers between devices: 82.1 us -> none  [the longest x1 42.5 us: body(): lax.all_gather(value_up, 'seq', axis=0, tiled=True)]
    unnamed x1 -> x0, blocking collectives: 34.9 us -> none
    psum x1 -> x0, blocking collectives: 33.4 us -> none  [body(): lax.psum(totals.astype(jnp.bfloat16), 'seq').astype(jnp.float32)]
    dot_general x8 -> x0, matrix products: 33.3 us -> none  [the longest x1 8.63 us: body(): jnp.einsum('bkgl,blkd->bkgd', softmax_terms, rebuilt_values, precision=TO...]
    pallas_call x0 -> x1, Pallas kernels: none -> 31.9 us  [fused_body(): pl.pallas_call(functools.partial(step_kernel, ns, nb), out_shape=jax.Shap...]
    pmax x1 -> x0, blocking collectives: 19.5 us -> none  [body(): upper_limit = jnp.maximum(lax.pmax(local_max, 'seq'), current_token_score)]
    all_gather x1 -> x0, blocking collectives: 5.21 us -> none  [body(): lax.all_gather(attended, 'batch', axis=0, tiled=True)]
    unnamed x13 -> x1, local copies, waits for them, and re-layouts: 5.55 us -> 1.3 us
  transfers between devices with their start and end apart: 2 -> 0, of which waited for: 2 -> 0; matrix products, arithmetic and copies ran while one was open for 2% -> 0% of each run, Pallas kernels for 0% -> 0%
where the time goes in v1:
time: 33.4 us; the launch traced here: 33.2 us
  Pallas kernels  31.9 us (96%)
  local copies, waits for them, and re-layouts  1.3 us (4%)
    pallas_call x1, Pallas kernels, fused_body(): pl.pallas_call(functools.partial(step_kernel, ns, nb), out_shape=jax.Shap...  31.9 us
    unnamed x1, local copies, waits for them, and re-layouts  1.3 us

profile of v1, /device:TPU:0, one launch (start us, length us, event | category | flops | bytes accessed | tf_op | source)
XLA Modules:
  0.0 33.2 jit_solution(4419892767635509766)
XLA Ops:
  0.0 31.9 %decode_step.1 = bf16[1,2048]{1,0:T(2,128)(2,1)} custom-call(s32[2]{0:T(128)} %lengths.1, bf16[2,64,128]{2,1,0:T(8,128)(2,1)} %query.1, bf16[2,2048,512]{2,1,0:T(8,128)(2,1)} %keys.1, bf16[2,2048,512]{2,1,0:T(8,128)(2,1)} %values.1, bf16[2,512]{1,0:T(2,128)(2,1)} %new_k.1, bf16[2,512]{1,0:T(2,128)(2,1)} %new_v.1, bf16[64,1024]{1,0:T(8,128)(2,1)} %key_up.1, ...), custom_call_target="tpu_custom_call" | custom-call | tf_op jit(solution)/shard_map/decode_step/pallas_call | solution.py:240
  31.9 1.3 %copy.11 = bf16[1,2048]{1,0:T(2,128)(2,1)} copy(bf16[1,2048]{1,0:T(2,128)(2,1)} %decode_step.1) | data formatting | bytes 8192

commit v2 on v1

--- a/solution.py
+++ b/solution.py
@@ -30,8 +30,8 @@
 
 def step_kernel(
     ns, nb, lengths, query, keys, values, new_k, new_v, key_up, value_up, out_w, out,
-    kbuf, vbuf, wbuf, qin, ku, nk, nv, qs, qfull, vcol, os, orecv, mls, mlrecv, att, ps, pr,
-    lsem, qsend, qrecv, vsend, vrecv, osend, orcv, msend, mrcv, asend, arcv, psend, prcv,
+    kbuf, vbuf, wbuf, qin, ku, nk, nv, qs, qfull, vcol, os, orecv, att, ps, pr,
+    lsem, qsend, qrecv, vsend, vrecv, osend, orcv, asend, arcv, psend, prcv,
 ):
     me = lax.axis_index("seq")
     mb = lax.axis_index("batch")
@@ -94,74 +94,97 @@
         )
 
     started = []
-
-    def send_all(count, index, axis, src_of, dst, send, recv):
-        for d in range(1, count):
-            target = lax.rem(index + d, count)
-            copy = hop(src_of(target), dst(index), send, recv, d, axis, target)
+    bits = [lax.rem(lax.div(me, 1 << i), 2) for i in range((ns - 1).bit_length())]
+
+    def across(d):
+        return sum((1 - x if d >> i & 1 else x) * (1 << i) for i, x in enumerate(bits))
+
+    def send_all(order, partner, index, axis, src_of, dst, send, recv):
+        for d in order:
+            copy = hop(src_of(partner(d)), dst(index), send, recv, d, axis, partner(d))
             copy.start()
             started.append(copy)
 
-    def receive(count, index, axis, src_of, dst, send, recv, d):
-        source = lax.rem(index + count - d, count)
-        hop(src_of(source), dst(source), send, recv, d, axis, source).wait_recv()
-
-    q_args = (ns, me, "seq", lambda t: qs.at[me], lambda s: qs.at[s], qsend, qrecv)
-    send_all(*q_args)
-
-    for d in range(1, ns):
-        receive(*q_args, d)
-
-    v_args = (
-        ns, me, "seq",
-        lambda t: value_up.at[:, pl.ds(pl.multiple_of(t * dh, 128), dh)],
-        lambda s: vcol.at[pl.ds(pl.multiple_of(s * rl, 8), rl)],
-        vsend, vrecv,
-    )
-    send_all(*v_args)
+    def receive(d, partner, axis, src_of, dst, send, recv):
+        hop(src_of(partner(d)), dst(partner(d)), send, recv, d, axis, partner(d)).wait_recv()
+
+    near, far = list(range(1, ns // 2)), list(range(ns // 2, ns))
+    everyone = near + far
+    q_src, q_dst = (lambda t: qs.at[me]), (lambda s: qs.at[s])
+    send_all(everyone, across, me, "seq", q_src, q_dst, qsend, qrecv)
 
     wide = lax.broadcasted_iota(jnp.int32, (heads, 2 * rl), 1) < rl
-    for pair in range(ns // 2):
-        even, odd = qs[2 * pair], qs[2 * pair + 1]
-        lanes = slice(pair * 2 * rl, (pair + 1) * 2 * rl)
-        qfull[0, :, lanes] = jnp.where(wide, even, pltpu.roll(odd, rl, 1))
-        qfull[1, :, lanes] = jnp.where(wide, pltpu.roll(even, rl, 1), odd)
+    side = lax.div(me, ns // 2)
+    half_rank = rl * ns // 2
+
+    def gathered(half):
+        for pair in range(ns // 4):
+            even = qs[half * (ns // 2) + 2 * pair]
+            odd = qs[half * (ns // 2) + 2 * pair + 1]
+            lanes = slice(pair * 2 * rl, (pair + 1) * 2 * rl)
+            qfull[0, half, :, lanes] = jnp.where(wide, even, pltpu.roll(odd, rl, 1))
+            qfull[1, half, :, lanes] = jnp.where(wide, pltpu.roll(even, rl, 1), odd)
+
+    def half_scores(b, half):
+        columns = pl.ds(pl.multiple_of(half * half_rank, 128), half_rank)
+        return split_dot(qfull[b, half], kbuf[b, :, columns], NT)
+
+    for d in near:
+        receive(d, across, "seq", q_src, q_dst, qsend, qrecv)
+    gathered(side)
+    early = []
+    for b in range(seqs):
+        local[5 + b].wait()
+        early.append(half_scores(b, side))
+    for d in far:
+        receive(d, across, "seq", q_src, q_dst, qsend, qrecv)
+    gathered(1 - side)
+
+    v_src = lambda t: value_up.at[:, pl.ds(pl.multiple_of(t * dh, 128), dh)]
+    v_dst = lambda s: vcol.at[pl.ds(pl.multiple_of(s * rl, 8), rl)]
+    send_all(everyone, across, me, "seq", v_src, v_dst, vsend, vrecv)
 
     positions = me * cache_len + lax.broadcasted_iota(jnp.int32, (1, cache_len), 1)
-    sums, tops, totals = [], [], []
+    lane = lax.broadcasted_iota(jnp.int32, (heads, 128), 1)
+    o_args = []
     for b in range(seqs):
         live = positions < lengths[b]
-        local[5 + b].wait()
-        scores = split_dot(qfull[b], kbuf[b], NT) * scale
+        scores = (early[b] + half_scores(b, 1 - side)) * scale
         scores = jnp.where(live, scores, NEGATIVE)
         top = jnp.max(scores, axis=1, keepdims=True)
         terms = jnp.where(live, jnp.exp(scores - top), 0.0)
-        tops.append(top)
-        totals.append(jnp.sum(terms, axis=1, keepdims=True))
+        total = jnp.sum(terms, axis=1, keepdims=True)
         local[7 + b].wait()
-        sums.append(split_dot(terms, vbuf[b], NN))
-
-    quarter = lax.broadcasted_iota(jnp.int32, (hl, 128), 1) // 32
-    for p in range(ns):
-        span = slice(p * hl, (p + 1) * hl)
-        os[p] = jnp.concatenate([x[span] for x in sums], axis=0).astype(BF16)
-        mls[p] = jnp.where(
-            quarter == 0, tops[0][span],
-            jnp.where(
-                quarter == 1, totals[0][span],
-                jnp.where(quarter == 2, tops[1][span], totals[1][span]),
-            ),
+        sums = split_dot(terms, vbuf[b], NN)
+        pieces = jnp.zeros((heads, 128), F32)
+        for at, value in ((0, top), (3, total)):
+            for k in range(3):
+                piece = value.astype(BF16).astype(F32)
+                pieces = jnp.where(lane == at + k, piece, pieces)
+                value = value - piece
+        packed = jnp.concatenate([sums, pieces], axis=1)
+        for p in range(ns):
+            os[b, p] = packed[p * hl : (p + 1) * hl].astype(BF16)
+        o_args.append(
+            (
+                "seq", lambda t, b=b: os.at[b, t], lambda s, b=b: orecv.at[b, s],
+                osend.at[b], orcv.at[b],
+            )
         )
-    m_args = (ns, me, "seq", lambda t: mls.at[t], lambda s: mlrecv.at[s], msend, mrcv)
-    o_args = (ns, me, "seq", lambda t: os.at[t], lambda s: orecv.at[s], osend, orcv)
-    send_all(*m_args)
-    send_all(*o_args)
+        send_all(everyone, across, me, *o_args[b])
+        orecv[b, me] = os[b, me]
 
     local[2].wait()
     local[3].wait()
     local[4].wait()
     mine = pl.ds(pl.multiple_of(me * hl, 8), hl)
-    own_query = jnp.concatenate([qfull[b, mine, :] for b in range(seqs)], axis=0)
+    own_query = jnp.concatenate(
+        [
+            jnp.concatenate([qfull[b, half, mine, :] for half in range(2)], axis=1)
+            for b in range(seqs)
+        ],
+        axis=0,
+    )
 
     def spread(ref):
         full = ref[...].astype(F32)
@@ -172,56 +195,58 @@
     own = jnp.sum(own_query * spread(nk), axis=1, keepdims=True) * scale
     fresh = spread(nv)
 
-    def stats(x):
-        return (
-            jnp.concatenate([x[:, 0:1], x[:, 64:65]], axis=0),
-            jnp.concatenate([x[:, 32:33], x[:, 96:97]], axis=0),
-        )
-
-    parts = [stats(mls[me])]
-    for d in range(1, ns):
-        receive(*m_args, d)
-        parts.append(stats(mlrecv[lax.rem(me + ns - d, ns)]))
-    limit = own
-    for top, _ in parts:
-        limit = jnp.maximum(limit, top)
-    own_weight = jnp.exp(own - limit)
-    latent = own_weight * fresh
-    below = own_weight
-    for d, (top, total) in enumerate(parts):
-        factor = jnp.exp(top - limit)
-        below = below + factor * total
-        if d:
-            receive(*o_args, d)
-            block = orecv[lax.rem(me + ns - d, ns)]
-        else:
-            block = os[me]
-        latent = latent + factor * block.astype(F32)
-    for d in range(1, ns):
-        receive(*v_args, d)
+    rank = nk.shape[1]
+    latents, belows = [], []
+    for b in range(seqs):
+        for d in near + far:
+            receive(d, across, *o_args[b])
+        span = slice(b * hl, (b + 1) * hl)
+        notes = orecv[b, :, :, rank:].astype(F32)
+        top = notes[:, :, 0:1] + notes[:, :, 1:2] + notes[:, :, 2:3]
+        total = notes[:, :, 3:4] + notes[:, :, 4:5] + notes[:, :, 5:6]
+        limit = jnp.maximum(jnp.max(top, axis=0), own[span])
+        factor = jnp.exp(top - limit[None])
+        own_weight = jnp.exp(own[span] - limit)
+        latent = own_weight * fresh[span]
+        for p in range(ns):
+            latent = latent + factor[p] * orecv[b, p, :, :rank].astype(F32)
+        latents.append(latent)
+        belows.append(own_weight + jnp.sum(factor * total, axis=0))
+    latent = jnp.concatenate(latents, axis=0)
+    below = jnp.concatenate(belows, axis=0)
+    for d in near + far:
+        receive(d, across, "seq", v_src, v_dst, vsend, vrecv)
     attended = split_dot(latent, vcol[...], NN) / below
     att[pl.ds(pl.multiple_of(mb * rows, 8), rows), :] = attended.astype(BF16).astype(F32)
 
     def att_rows(i):
         return att.at[pl.ds(pl.multiple_of(i * rows, 8), rows)]
 
-    a_args = (nb, mb, "batch", lambda t: att_rows(mb), att_rows, asend, arcv)
-    send_all(*a_args)
+    def turned(d):
+        return lax.rem(mb + d, nb)
+
+    def turned_back(d):
+        return lax.rem(mb + nb - d, nb)
+
+    a_src = lambda t: att_rows(mb)
+    send_all(range(1, nb), turned, mb, "batch", a_src, att_rows, asend, arcv)
     for d in range(1, nb):
-        receive(*a_args, d)
+        receive(d, turned_back, "batch", a_src, att_rows, asend, arcv)
     features = jnp.concatenate(
         [att[pl.ds(g, nb * seqs, stride=hl), :] for g in range(hl)], axis=1
     ).astype(BF16)
     local[9].wait()
     product = lax.dot_general(features, wbuf[...], NN, preferred_element_type=F32)
     for p in range(ns):
-        ps[p] = product[p : p + 1]
-    p_args = (ns, me, "seq", lambda t: ps.at[t], lambda s: pr.at[s], psend, prcv)
-    send_all(*p_args)
-    result = ps[me]
-    for d in range(1, ns):
-        receive(*p_args, d)
-        result = result + pr[lax.rem(me + ns - d, ns)]
+        ps[p] = product[p : p + 1].astype(ps.dtype)
+    p_src, p_dst = (lambda t: ps.at[t]), (lambda s: pr.at[s])
+    send_all(everyone, across, me, "seq", p_src, p_dst, psend, prcv)
+    pr[me] = ps[me]
+    for d in near + far:
+        receive(d, across, "seq", p_src, p_dst, psend, prcv)
+    result = pr[0].astype(F32)
+    for p in range(1, ns):
+        result = result + pr[p].astype(F32)
     out[...] = result.astype(out.dtype)
     for copy in started:
         copy.wait_send()
@@ -251,18 +276,17 @@
             pltpu.VMEM(new_keys.shape, BF16),
             pltpu.VMEM(new_values.shape, BF16),
             pltpu.VMEM((ns, heads, seqs * key_up.shape[0]), F32),
-            pltpu.VMEM((seqs, heads, rank), F32),
+            pltpu.VMEM((seqs, 2, heads, rank // 2), F32),
             pltpu.VMEM((rank, dh), BF16),
-            pltpu.VMEM((ns, seqs * hl, rank), BF16),
-            pltpu.VMEM((ns, seqs * hl, rank), BF16),
-            pltpu.VMEM((ns, hl, 128), F32),
-            pltpu.VMEM((ns, hl, 128), F32),
+            pltpu.VMEM((seqs, ns, hl, rank + 128), BF16),
+            pltpu.VMEM((seqs, ns, hl, rank + 128), BF16),
             pltpu.VMEM((nb * seqs * hl, dh), F32),
-            pltpu.VMEM((ns, 1, width), F32),
-            pltpu.VMEM((ns, 1, width), F32),
+            pltpu.VMEM((ns, 1, width), BF16),
+            pltpu.VMEM((ns, 1, width), BF16),
             sem((10,)),
         ]
-        + [sem((ns,))] * 8
+        + [sem((ns,))] * 4
+        + [sem((seqs, ns))] * 2
         + [sem((nb,))] * 2
         + [sem((ns,))] * 2,
         compiler_params=pltpu.CompilerParams(collective_id=0, has_side_effects=True),

time: 33.4 us -> 32.1 us (0.961)
  Pallas kernels: 31.9 us -> 30.6 us
    pallas_call x1, Pallas kernels: 31.9 us -> 30.6 us  [fused_body(): pl.pallas_call(functools.partial(step_kernel, ns, nb), out_shape=jax.Shap...]
where the time goes in v2:
time: 32.1 us; the launch traced here: 31.9 us
  Pallas kernels  30.6 us (95%)
  local copies, waits for them, and re-layouts  1.3 us (4%)
    pallas_call x1, Pallas kernels, fused_body(): pl.pallas_call(functools.partial(step_kernel, ns, nb), out_shape=jax.Shap...  30.6 us
    unnamed x1, local copies, waits for them, and re-layouts  1.3 us

profile of v2, /device:TPU:0, one launch (start us, length us, event | category | flops | bytes accessed | tf_op | source)
XLA Modules:
  0.0 31.9 jit_solution(2111901689218607435)
XLA Ops:
  0.0 30.6 %decode_step.1 = bf16[1,2048]{1,0:T(2,128)(2,1)} custom-call(s32[2]{0:T(128)} %lengths.1, bf16[2,64,128]{2,1,0:T(8,128)(2,1)} %query.1, bf16[2,2048,512]{2,1,0:T(8,128)(2,1)} %keys.1, bf16[2,2048,512]{2,1,0:T(8,128)(2,1)} %values.1, bf16[2,512]{1,0:T(2,128)(2,1)} %new_k.1, bf16[2,512]{1,0:T(2,128)(2,1)} %new_v.1, bf16[64,1024]{1,0:T(8,128)(2,1)} %key_up.1, ...), custom_call_target="tpu_custom_call" | custom-call | tf_op jit(solution)/shard_map/decode_step/pallas_call | solution.py:265
  30.6 1.3 %copy.11 = bf16[1,2048]{1,0:T(2,128)(2,1)} copy(bf16[1,2048]{1,0:T(2,128)(2,1)} %decode_step.1) | data formatting | bytes 8192
